TPU v7x, 256 devices: a whole 4x4x8 slice. The times are simulated.
256 devices in a mesh: pb: 4 (over x_hi, core), db: 64 (over x_lo, y, z).
Axes of the slice: x: 4 (x_hi: 2, x_lo: 2; x = x_hi * 2 + x_lo), y: 4, z: 8, core: 2. Of those that a mesh axis runs over, the one named last changes fastest.
Arguments:
- queries: bfloat16 [1024, 1024], P(('pb', 'db')), may hold values from -6 to 6
- residual: bfloat16 [65536, 1024], P('db'), may hold values from -3 to 3
- codes: int32 [65536, 64], P('db'), may hold values from 0 to 255
- codebook: float32 [64, 256, 16], replicated, may hold values from -6 to 6
- ranks: int32 [1024], P(('pb', 'db')), may hold values from 0 to 63
Outputs:
- hits: float32 [3, 1024], P(None, ('pb', 'db'))
- totals: float32 [3], replicated
All inputs are finite; a program needn't handle non-finite values.
Results may differ from a plain program's by a relative error of at most 0.00035.
Values may be sent and summed in bfloat16 or wider, within the bound.
A program may use at most 128 MiB of HBM per device.

v0:
```python
import jax
import jax.numpy as jnp
from jax import lax
from jax.sharding import Mesh
from jax.sharding import PartitionSpec as P

LEVELS = 64
DB = ("db_0", "db_1", "db_2")
PB = ("pb_0", "pb_1")
PB_DB = ("pb_0", "pb_1", "db_0", "db_1", "db_2")


def in_one_piece(arrays, axis, dim, along):
    columns = [a.reshape(*a.shape[:along], -1) for a in arrays]
    both = jnp.concatenate(columns, axis=along)
    result, at, done = (lax.all_gather(both, axis, axis=dim, tiled=True), 0, [])
    for a, column in zip(arrays, columns):
        piece = result[..., at : at + column.shape[along]]
        done.append(piece.reshape(*piece.shape[:along], *a.shape[along:]))
        at += column.shape[along]
    return tuple(done)


def split_up(array, dim, length):
    before, after = (array.shape[:dim], array.shape[dim + 1 :])
    return jnp.moveaxis(array.reshape(*before, length, -1, *after), dim, 0)


def sent_and_summed(array, axis, dim):
    length = lax.axis_size(axis)
    parts = lax.all_to_all(split_up(array, dim, length), axis, 0, 0, tiled=True)
    return jnp.sum(parts, axis=0)


def by_axis(array, axes):
    for axis in axes:
        array = lax.psum(array, axis)
    return array


def pq_lookup(queries, centre_high, centre_low, centre_norms):
    count = queries.shape[0]
    subspaces, centroids, subdim = centre_high.shape
    size = 64

    def one_group(group):
        parts = group.reshape(size, subspaces, subdim)
        query_parts = jnp.sum(parts.astype(jnp.float32) ** 2, axis=-1)
        cross = jnp.einsum("qmj,mcj->qmc", parts, centre_high, preferred_element_type=jnp.float32)
        cross = cross + jnp.einsum(
            "qmj,mcj->qmc", parts, centre_low, preferred_element_type=jnp.float32
        )
        lookup = (query_parts[:, :, None] + centre_norms[None] - 2.0 * cross) / (subspaces * subdim)
        return lookup.astype(jnp.bfloat16).reshape(size, subspaces * centroids)

    tables = lax.map(one_group, queries.reshape(count // size, size, queries.shape[1]))
    return tables.reshape(count, subspaces * centroids)


def block_hits(queries, query_norms, lookup, bounds, vectors, code_values, centroids):
    width = vectors.shape[1]
    size = vectors.shape[0]
    vector_norms = jnp.sum(vectors.astype(jnp.float32) ** 2, axis=1)
    cross = lax.dot_general(
        queries, vectors, (((1,), (1,)), ((), ())), preferred_element_type=jnp.float32
    )
    exact = (query_norms[:, None] + vector_norms[None, :] - 2.0 * cross) / width
    levels = jnp.arange(centroids, dtype=jnp.bfloat16)
    one_hot = (code_values[:, :, None] == levels).astype(jnp.bfloat16).reshape(size, -1)
    coarse = lax.dot_general(
        lookup, one_hot, (((1,), (1,)), ((), ())), preferred_element_type=jnp.float32
    )
    exact_hit = jax.nn.sigmoid((bounds[:, None] - exact) / 0.02)
    coarse_hit = jax.nn.sigmoid((bounds[:, None] - coarse) / 0.02)
    return jnp.stack(
        [jnp.sum(exact_hit, 1), jnp.sum(coarse_hit, 1), jnp.sum(exact_hit * coarse_hit, 1)]
    )


def sweep(counts, vectors, code_values, queries, query_norms, lookup, bounds, centroids):
    total = vectors.shape[0]
    size = 128
    blocks = total // size
    vector_blocks = vectors.reshape(blocks, size, vectors.shape[1])
    code_blocks = code_values.reshape(blocks, size, code_values.shape[1])

    def absorb_block(carry, item):
        return (
            carry + block_hits(queries, query_norms, lookup, bounds, item[0], item[1], centroids),
            None,
        )

    counts, _ = lax.scan(absorb_block, counts, (vector_blocks, code_blocks))
    return counts


def per_device(queries, residual, codes, codebook, ranks):
    count = queries.shape[0]
    rows_count = residual.shape[0]
    centroids = codebook.shape[1]
    centre_ids = jnp.arange(centroids, dtype=jnp.int32)
    selector = (codes[:, :, None] == centre_ids).astype(jnp.float32)
    recon = jnp.einsum("rmc,mcj->rmj", selector, codebook, precision=lax.Precision.HIGHEST).reshape(
        rows_count, -1
    )
    vectors = (recon + residual.astype(jnp.float32)).astype(jnp.bfloat16)
    code_values = codes.astype(jnp.bfloat16)
    rank_values = ranks.astype(jnp.bfloat16)
    centre_high = codebook.astype(jnp.bfloat16)
    centre_low = (codebook - centre_high.astype(jnp.float32)).astype(jnp.bfloat16)
    centre_norms = jnp.sum(codebook * codebook, axis=-1)
    visiting, visiting_ranks = in_one_piece((queries, rank_values), DB, 0, 1)
    lookup = pq_lookup(visiting, centre_high, centre_low, centre_norms)
    bounds = 1.9 + 0.6 * visiting_ranks.astype(jnp.float32) / (LEVELS - 1)
    visiting_norms = jnp.sum(visiting.astype(jnp.float32) ** 2, axis=1)
    empty = jnp.zeros((3, visiting.shape[0]), jnp.float32)
    partial_value = sweep(
        empty, vectors, code_values, visiting, visiting_norms, lookup, bounds, centroids
    )
    database = rows_count * lax.axis_size(DB)
    everyone = count * lax.axis_size(PB) * lax.axis_size(DB)
    hits = sent_and_summed(partial_value, DB, 1) / database
    totals = by_axis(jnp.sum(hits, axis=1), PB_DB) / everyone
    return (hits, totals)


def solution(mesh):
    finer = Mesh(mesh.devices.reshape(2, 2, 2, 4, 8), ("pb_0", "pb_1", "db_0", "db_1", "db_2"))
    return jax.shard_map(
        per_device,
        mesh=finer,
        in_specs=(P(PB_DB, None), P(DB, None), P(DB, None), P(), P(PB_DB)),
        out_specs=(P(None, PB_DB), P()),
        check_vma=False,
    )
```

profile of v0, /device:TPU:1, one launch (start us, length us, event | category | flops | bytes accessed | tf_op | source)
XLA Modules:
  0.0 376.0 jit_solution(2083742981077836375)
XLA Ops:
  2.2 134.9 %all-gather = bf16[64,4,1025]{2,1,0:T(4,128)(2,1)S(1)} all-gather(bf16[1,4,1025]{2,1,0:T(4,128)(2,1)S(1)} %maximum_bitcast_fusion), channel_id=1, replica_groups=mesh['pb_0'=2,'pb_1'=2,'db_0'=2,'db_1'=4,'db_2'=8] {'db_0','db_1','db_2'}, dimensions={0}, use_global_device_ids=true | all-gather | bytes 533000 | tf_op jit(solution)/shard_map/all_gather | solution.py:16
  138.6 2.0 subtract_convert_fusion
  140.6 35.1 %fusion.36 = f32[64,1024,16]{1,2,0:T(8,128)} fusion(f32[64,256,16]{1,2,0:T(8,128)S(1)} %copy-done.1, s32[1024,64]{0,1:T(8,128)S(1)} %copy-done.2), kind=kOutput, calls=%fused_computation.35 | convolution fusion | flops 3238002688 | bytes 5505024 | tf_op jit(solution)/shard_map/rmc,mcj->rmj/dot_general | solution.py:103
  175.7 41.7 %while.21 = (s32[]{:T(128)}, bf16[4,64,16384]{2,1,0:T(8,128)(2,1)}, bf16[4,64,1024]{2,1,0:T(8,128)(2,1)}, f32[64,256]{1,0:T(8,128)S(1)}, bf16[64,256,16]{1,2,0:T...) while((s32[]{:T(128)}, bf16[4,64,16384]{2,1,0:T(8,128)(2,1)}, bf16[4,64,1024]{2,1,0:T(8,128)(2,1)}, ...), condition=%wide.region_4.5_spmd, body=%wide.region_2.4_spmd.sunk | while | flops 73592832 | bytes 25133648 | solution.py:56
  177.7 1.5 fusion.65
  179.2 2.6 copy.30
  181.8 2.9 broadcast_in_dim.13
  184.6 1.5 constant_dynamic-update-slice_fusion.2
  188.1 1.5 fusion.65
  189.7 2.6 copy.30
  192.2 2.9 broadcast_in_dim.13
  195.1 1.4 constant_dynamic-update-slice_fusion.2
  198.5 1.5 fusion.65
  200.0 2.6 copy.30
  202.6 2.9 broadcast_in_dim.13
  205.5 1.5 constant_dynamic-update-slice_fusion.2
  208.9 1.5 fusion.65
  210.5 2.6 copy.30
  213.0 2.9 broadcast_in_dim.13
  215.9 1.5 constant_dynamic-update-slice_fusion.2
  217.4 5.4 %copy.18 = f32[1024,1024]{1,0:T(8,128)} copy(f32[1024,1024]{0,1:T(8,128)} %bitcast.108) | data formatting | bytes 8388608 | tf_op jit(solution)/shard_map/reshape | solution.py:103
  222.9 3.6 add_convert_fusion
  226.6 73.5 %while.22 = (s32[]{:T(128)}, f32[3,256]{1,0:T(4,128)S(1)}, f32[256]{0:T(256)S(1)}, f32[256]{0:T(256)S(1)}, bf16[8,128,1024]{2,1,0:T(8,128)(2,1)S(1)}, /*index=5*...) while((s32[]{:T(128)}, f32[3,256]{1,0:T(4,128)S(1)}, ...), condition=%wide.region_10.11_spmd.clone, body=%wide.region_5.10_spmd.clone.sunk | while | flops 1143933056 | bytes 60227732 | solution.py:93
  227.9 3.0 copy.31
  231.2 2.9 fusion.68
  234.3 1.4 fusion.69
  237.0 3.0 copy.31
  240.4 2.9 fusion.68
  243.5 1.4 fusion.69
  246.2 3.0 copy.31
  249.6 2.9 fusion.68
  252.7 1.4 fusion.69
  255.4 3.0 copy.31
  258.8 2.9 fusion.68
  264.6 3.0 copy.31
  268.0 2.9 fusion.68
  273.8 3.0 copy.31
  277.2 2.9 fusion.68
  283.0 3.0 copy.31
  286.4 2.9 fusion.68
  292.2 3.0 copy.31
  295.5 2.9 fusion.68
  300.3 13.8 %all_to_all.5 = f32[64,3,4]{2,1,0:T(4,128)S(1)} all-to-all(f32[64,3,4]{2,1,0:T(4,128)S(1)} %copy.21), channel_id=1, replica_groups=mesh['pb_0'=2,'pb_1'=2,'db_0'=2,'db_1'=4,'db_2'=8] {'db_0','db_1','db_2'}, dimensions={0} | all-to-all | bytes 6144 | tf_op jit(solution)/shard_map/all_to_all | solution.py:31
  314.8 5.3 %psum.35 = f32[3]{0:T(128)S(1)} all-reduce(f32[3]{0:T(128)S(1)} %get-tuple-element.153), channel_id=1, replica_groups=mesh['pb_0'=2,'pb_1'=2,'db_0'=2,'db_1'=4,'db_2'=8] {'pb_0'}, use_global_device_ids=true, to_apply=%region_13.14 | all-reduce | flops 3 | bytes 24 | tf_op jit(solution)/shard_map/psum | solution.py:37
  320.1 33.2 %psum.36 = f32[3]{0:T(128)S(1)} all-reduce(f32[3]{0:T(128)S(1)} %psum.35), channel_id=1, replica_groups=mesh['pb_0'=2,'pb_1'=2,'db_0'=2,'db_1'=4,'db_2'=8] {'pb_1'}, use_global_device_ids=true, to_apply=%region_14.15 | all-reduce | flops 3 | bytes 24 | tf_op jit(solution)/shard_map/psum | solution.py:37
  353.3 3.8 psum.37
  357.1 7.4 %psum.38 = f32[3]{0:T(128)S(1)} all-reduce(f32[3]{0:T(128)S(1)} %psum.37), channel_id=1, replica_groups=mesh['pb_0'=2,'pb_1'=2,'db_0'=2,'db_1'=4,'db_2'=8] {'db_1'}, use_global_device_ids=true, to_apply=%region_16.17 | all-reduce | flops 3 | bytes 24 | tf_op jit(solution)/shard_map/psum | solution.py:37
  364.4 11.1 %psum.39 = f32[3]{0:T(128)S(1)} all-reduce(f32[3]{0:T(128)S(1)} %psum.38), channel_id=1, replica_groups=mesh['pb_0'=2,'pb_1'=2,'db_0'=2,'db_1'=4,'db_2'=8] {'db_2'}, use_global_device_ids=true, to_apply=%region_17.18 | all-reduce | flops 3 | bytes 24 | tf_op jit(solution)/shard_map/psum | solution.py:37
  (105 shorter events, 34.0 us)
Async XLA Ops:
  0.6 139.9 %copy-start.1 = (f32[64,256,16]{1,2,0:T(8,128)S(1)}, f32[64,256,16]{1,2,0:T(8,128)}, u32[]{:S(2)}) copy-start(f32[64,256,16]{1,2,0:T(8,128)} %param.12) | copy-start | bytes 3145732
  0.6 139.9 %copy-start.2 = (s32[1024,64]{0,1:T(8,128)S(1)}, s32[1024,64]{0,1:T(8,128)}, u32[]{:S(2)}) copy-start(s32[1024,64]{0,1:T(8,128)} %param.11) | copy-start | bytes 786436
  227.9 3.4 copy-start
  237.0 3.4 copy-start
  246.2 3.4 copy-start
  255.4 3.4 copy-start
  264.6 3.4 copy-start
  273.8 3.4 copy-start
  283.0 3.4 copy-start
  292.2 3.4 copy-start
where the time goes:
time: 383 us; the launch traced here: 376 us
  blocking collectives  209 us (55%)
  matrix products  78.9 us (21%)
  local copies, waits for them, and re-layouts  75.8 us (20%)
  other arithmetic  10.5 us (3%)
    all_gather x1, blocking collectives, in_one_piece(): result, at, done = (lax.all_gather(both, axis, axis=dim, tiled=True), 0, [])  135 us
    psum x5, blocking collectives, by_axis(): array = lax.psum(array, axis)  60.6 us
    dot_general x1, matrix products, per_device(): jnp.einsum('rmc,mcj->rmj', selector, codebook, precision=lax.Precision.HI...  35.1 us
    while x40, local copies, waits for them, and re-layouts  26.8 us
    dot_general x8, matrix products, block_hits(): lax.dot_general(lookup, one_hot, (((1,), (1,)), ((), ())), preferred_elem...  23.5 us
    all_to_all x1, blocking collectives, sent_and_summed(): parts = lax.all_to_all(split_up(array, dim, length), axis, 0, 0, tiled=True)  13.8 us
    broadcast_in_dim x4, local copies, waits for them, and re-layouts, pq_lookup(): lax.map(one_group, queries.reshape(count // size, size, queries.shape[1]))  11.5 us
    dot_general x8, matrix products, block_hits(): lax.dot_general(queries, vectors, (((1,), (1,)), ((), ())), preferred_ele...  11.2 us

commit v1 on v0

v1 whole, which is shorter than its diff:
```python
import jax
import jax.numpy as jnp
from jax import lax
from jax.experimental import pallas as pl
from jax.experimental.pallas import tpu as pltpu
from jax.sharding import PartitionSpec as P

LEVELS = 64
SHARP = 50.0
LANES = 128
MESH = pl.DeviceIdType.MESH


def kernel_body(
    sizes,
    ranks_ref,
    queries_ref,
    residual_ref,
    codes_ref,
    codebook_ref,
    hits_ref,
    totals_ref,
    message,
    arrived,
    table,
    codes,
    residual,
    vectors,
    recon_high,
    recon_low,
    vector_bias,
    recon_bias,
    visiting,
    query_bias,
    sums,
    leaving,
    returned,
    own_sums,
    group_sums,
    local_sems,
    query_send,
    query_recv,
    hit_send,
    hit_recv,
    total_send,
    total_recv,
):
    db, pb, rows, width, database, everyone, subdim = sizes
    count = queries_ref.shape[0]
    me = lax.axis_index("db")
    my_pb = lax.axis_index("pb")

    loads = [
        pltpu.make_async_copy(codebook_ref, table, local_sems.at[0]),
        pltpu.make_async_copy(codes_ref, codes, local_sems.at[1]),
        pltpu.make_async_copy(residual_ref, residual, local_sems.at[2]),
    ]
    for load in loads:
        load.start()

    barrier = pltpu.get_barrier_semaphore()

    def greet(step, _):
        peer = lax.rem(me + step, db)
        pl.semaphore_signal(barrier, inc=1, device_id={"db": peer}, device_id_type=MESH)
        return 0

    lax.fori_loop(1, db, greet, 0)
    for step in range(1, pb):
        peer = lax.rem(my_pb + step, pb)
        pl.semaphore_signal(barrier, inc=1, device_id={"pb": peer}, device_id_type=MESH)

    message[:, :width] = queries_ref[...]
    row_ids = lax.broadcasted_iota(jnp.int32, (count, LANES), 0)
    rank_block = jnp.zeros((count, LANES), jnp.float32)
    for row in range(count):
        rank_block = jnp.where(row_ids == row, ranks_ref[row].astype(jnp.float32), rank_block)
    message[:, width:] = rank_block.astype(jnp.bfloat16)
    arrived[0] = message[...]

    pl.semaphore_wait(barrier, db - 1 + pb - 1)

    def send_queries(step, _):
        peer = lax.rem(me + step, db)
        pltpu.make_async_remote_copy(
            src_ref=message,
            dst_ref=arrived.at[step],
            send_sem=query_send,
            recv_sem=query_recv,
            device_id={"db": peer},
            device_id_type=MESH,
        ).start()
        return 0

    lax.fori_loop(1, db, send_queries, 0)

    for load in loads:
        load.wait()

    group = LANES // subdim

    def prepare(index, _):
        at, part = index // (width // LANES), lax.rem(index, width // LANES)
        n_at = pl.multiple_of(at * LANES, LANES)
        d_at = pl.multiple_of(part * LANES, LANES)
        extra = residual[pl.ds(n_at, LANES), pl.ds(d_at, LANES)].astype(jnp.float32).T
        chosen = codes[pl.ds(pl.multiple_of(part * group, group), group), pl.ds(n_at, LANES)]
        vector_norm = jnp.zeros((8, LANES), jnp.float32)
        recon_norm = jnp.zeros((8, LANES), jnp.float32)
        for inner in range(group):
            pick = jnp.broadcast_to(chosen[inner : inner + 1, :], (subdim, LANES))
            low_pick = pick & (LANES - 1)
            entries = table[part * group + inner]
            below = jnp.take_along_axis(
                entries[:, :LANES], low_pick, axis=1, mode="promise_in_bounds"
            )
            above = jnp.take_along_axis(
                entries[:, LANES:], low_pick, axis=1, mode="promise_in_bounds"
            )
            recon = jnp.where(pick >= LANES, above, below)
            vector = (recon + extra[inner * subdim : (inner + 1) * subdim, :]).astype(jnp.bfloat16)
            high = recon.astype(jnp.bfloat16)
            low = (recon - high.astype(jnp.float32)).astype(jnp.bfloat16)
            here = pl.ds(pl.multiple_of(d_at + inner * subdim, subdim), subdim)
            vectors[here, pl.ds(n_at, LANES)] = vector
            recon_high[here, pl.ds(n_at, LANES)] = high
            recon_low[here, pl.ds(n_at, LANES)] = low
            wide = vector.astype(jnp.float32)
            squares = wide * wide
            vector_norm += squares[:8] + squares[8:]
            squares = recon * recon
            recon_norm += squares[:8] + squares[8:]

        @pl.when(part == 0)
        def _():
            vector_bias[:, pl.ds(n_at, LANES)] = jnp.zeros((8, LANES), jnp.float32)
            recon_bias[:, pl.ds(n_at, LANES)] = jnp.zeros((8, LANES), jnp.float32)

        vector_bias[:, pl.ds(n_at, LANES)] += vector_norm
        recon_bias[:, pl.ds(n_at, LANES)] += recon_norm
        return 0

    lax.fori_loop(0, (rows // LANES) * (width // LANES), prepare, 0)

    scale = SHARP / 2
    vector_row = jnp.sum(vector_bias[...], axis=0, keepdims=True) * (-scale / width)
    recon_row = jnp.sum(recon_bias[...], axis=0, keepdims=True) * (-scale / width)
    vector_bias[...] = jnp.broadcast_to(vector_row, vector_bias.shape)
    recon_bias[...] = jnp.broadcast_to(recon_row, recon_bias.shape)

    incoming = arrived.at[pl.ds(1, db - 1)]
    pltpu.make_async_copy(incoming, incoming, query_recv).wait()

    stack = 16 // count

    def unpack(index, _):
        blocks = [arrived[index * stack + i].astype(jnp.float32) for i in range(stack)]
        block = jnp.concatenate(blocks, axis=0)
        here = pl.ds(pl.multiple_of(index * 16, 16), 16)
        own = block[:, :width]
        visiting[here, :] = own.astype(jnp.bfloat16)
        norm = jnp.sum(own * own, axis=1, keepdims=True)
        bound = 1.9 + 0.6 * block[:, width:] / (LEVELS - 1)
        query_bias[here, :] = scale * bound - (scale / width) * norm
        return 0

    lax.fori_loop(0, db // stack, unpack, 0)

    total = db * count
    sums[...] = jnp.zeros_like(sums)
    tile = 256

    def absorb(index, _):
        n_at = pl.ds(pl.multiple_of(index * tile, tile), tile)
        mine = visiting[...]
        cross = jnp.dot(mine, vectors[:, n_at], preferred_element_type=jnp.float32)
        coarse_cross = jnp.dot(mine, recon_high[:, n_at], preferred_element_type=jnp.float32)
        coarse_cross += jnp.dot(mine, recon_low[:, n_at], preferred_element_type=jnp.float32)
        bias = query_bias[...]
        for half in range(tile // LANES):
            lanes = slice(half * LANES, (half + 1) * LANES)
            row_at = pl.ds(pl.multiple_of(index * tile + half * LANES, LANES), LANES)
            exact = bias + vector_bias[0:1, row_at] + cross[:, lanes] * (2 * scale / width)
            coarse = bias + recon_bias[0:1, row_at] + coarse_cross[:, lanes] * (2 * scale / width)
            exact_hit = 0.5 * jnp.tanh(exact) + 0.5
            coarse_hit = 0.5 * jnp.tanh(coarse) + 0.5
            sums[0] += exact_hit
            sums[1] += coarse_hit
            sums[2] += exact_hit * coarse_hit
        return 0

    lax.fori_loop(0, rows // tile, absorb, 0)

    lane = lax.broadcasted_iota(jnp.int32, (total, LANES), 1)
    place = lax.rem(lax.broadcasted_iota(jnp.int32, (total, LANES), 0), count)
    spread = jnp.zeros((total, LANES), jnp.float32)
    for kind in range(3):
        column = jnp.sum(sums[kind], axis=1, keepdims=True)
        spread = jnp.where(lane == count * kind + place, column, spread)
        spread = jnp.where(lane == 3 * count + kind, column, spread)
    folder = (
        lax.broadcasted_iota(jnp.int32, (db, total), 1) // count
        == lax.broadcasted_iota(jnp.int32, (db, total), 0)
    ).astype(jnp.float32)
    folded = jnp.dot(
        folder, spread, preferred_element_type=jnp.float32, precision=lax.Precision.HIGHEST
    )
    overall = jnp.sum(spread, axis=0, keepdims=True)
    short_lane = lax.broadcasted_iota(jnp.int32, (db, LANES), 1)
    folded = jnp.where(short_lane < 3 * count, folded, overall)
    leaving[...] = folded.reshape(db, 1, LANES)
    returned[0] = folded[0:1, :]

    def send_hits(step, _):
        peer = lax.rem(me + db - step, db)
        pltpu.make_async_remote_copy(
            src_ref=leaving.at[step],
            dst_ref=returned.at[step],
            send_sem=hit_send,
            recv_sem=hit_recv,
            device_id={"db": peer},
            device_id_type=MESH,
        ).start()
        return 0

    lax.fori_loop(1, db, send_hits, 0)
    landing = returned.at[pl.ds(1, db - 1)]
    pltpu.make_async_copy(landing, landing, hit_recv).wait()
    mine = jnp.sum(returned[...], axis=0)
    own_sums[...] = mine
    for step in range(1, pb):
        pltpu.make_async_remote_copy(
            src_ref=own_sums,
            dst_ref=group_sums.at[step - 1],
            send_sem=total_send,
            recv_sem=total_recv,
            device_id={"pb": lax.rem(my_pb + step, pb)},
            device_id_type=MESH,
        ).start()
    for kind in range(3):
        hits_ref[kind : kind + 1, :] = mine[:, kind * count : (kind + 1) * count] * (1.0 / database)
    pltpu.make_async_copy(group_sums, group_sums, total_recv).wait()
    all_sums = mine + jnp.sum(group_sums[...], axis=0)
    totals_ref[...] = all_sums[:, 3 * count : 3 * count + 3] * (1.0 / (database * everyone))

    pltpu.make_async_copy(incoming, incoming, query_send).wait()
    pltpu.make_async_copy(landing, landing, hit_send).wait()
    pltpu.make_async_copy(group_sums, group_sums, total_send).wait()


def solution(mesh):
    db, pb = mesh.shape["db"], mesh.shape["pb"]

    def per_device(queries, residual, codes, codebook, ranks):
        count, width = queries.shape
        rows = residual.shape[0]
        subspaces, centroids, subdim = codebook.shape
        sizes = (db, pb, rows, width, rows * db, count * pb * db, subdim)
        total = db * count
        in_vmem = pl.BlockSpec(memory_space=pltpu.VMEM)
        anywhere = pl.BlockSpec(memory_space=pl.ANY)
        dma = pltpu.SemaphoreType.DMA
        hits, totals = pl.pallas_call(
            lambda *refs: kernel_body(sizes, *refs),
            out_shape=(
                jax.ShapeDtypeStruct((3, count), jnp.float32),
                jax.ShapeDtypeStruct((1, 3), jnp.float32),
            ),
            in_specs=[
                pl.BlockSpec(memory_space=pltpu.SMEM),
                in_vmem,
                anywhere,
                anywhere,
                anywhere,
            ],
            out_specs=(in_vmem, in_vmem),
            scratch_shapes=[
                pltpu.VMEM((count, width + LANES), jnp.bfloat16),
                pltpu.VMEM((db, count, width + LANES), jnp.bfloat16),
                pltpu.VMEM((subspaces, subdim, centroids), jnp.float32),
                pltpu.VMEM((subspaces, rows), jnp.int32),
                pltpu.VMEM((rows, width), jnp.bfloat16),
                pltpu.VMEM((width, rows), jnp.bfloat16),
                pltpu.VMEM((width, rows), jnp.bfloat16),
                pltpu.VMEM((width, rows), jnp.bfloat16),
                pltpu.VMEM((8, rows), jnp.float32),
                pltpu.VMEM((8, rows), jnp.float32),
                pltpu.VMEM((total, width), jnp.bfloat16),
                pltpu.VMEM((total, LANES), jnp.float32),
                pltpu.VMEM((3, total, LANES), jnp.float32),
                pltpu.VMEM((db, 1, LANES), jnp.float32),
                pltpu.VMEM((db, 1, LANES), jnp.float32),
                pltpu.VMEM((1, LANES), jnp.float32),
                pltpu.VMEM((pb - 1, 1, LANES), jnp.float32),
                dma((3,)),
                dma,
                dma,
                dma,
                dma,
                dma,
                dma,
            ],
            compiler_params=pltpu.CompilerParams(
                collective_id=0, has_side_effects=True, vmem_limit_bytes=60 * 1024 * 1024
            ),
            name="recall",
        )(ranks, queries, residual, codes.T, jnp.transpose(codebook, (0, 2, 1)))
        return hits, totals.reshape(3)

    return jax.shard_map(
        per_device,
        mesh=mesh,
        in_specs=(P(("pb", "db"), None), P("db", None), P("db", None), P(), P(("pb", "db"))),
        out_specs=(P(None, ("pb", "db")), P()),
        check_vma=False,
    )
```

time: 383 us -> 49.1 us (0.13); the launches traced: 376 us -> 48.9 us
  blocking collectives: 209 us -> 0 us
  matrix products: 78.9 us -> 0 us
  local copies, waits for them, and re-layouts: 75.8 us -> 2.39 us
  Pallas kernels: 0 us -> 45.9 us
  other arithmetic: 10.5 us -> 0 us
    all_gather x1 -> x0, blocking collectives: 135 us -> none  [in_one_piece(): result, at, done = (lax.all_gather(both, axis, axis=dim, tiled=True), 0, [])]
    dot_general x25 -> x0, matrix products: 78.9 us -> none  [the longest x1 35.1 us: per_device(): jnp.einsum('rmc,mcj->rmj', selector, codebook, precision=lax.Precision.HI...]
    psum x5 -> x0, blocking collectives: 60.6 us -> none  [by_axis(): array = lax.psum(array, axis)]
    pallas_call x0 -> x1, Pallas kernels: none -> 45.9 us  [per_device(): pl.pallas_call(lambda *refs: kernel_body(sizes, *refs), out_shape=(jax.Sh...]
    while x40 -> x0, local copies, waits for them, and re-layouts: 26.8 us -> none
    all_to_all x1 -> x0, blocking collectives: 13.8 us -> none  [sent_and_summed(): parts = lax.all_to_all(split_up(array, dim, length), axis, 0, 0, tiled=True)]
    broadcast_in_dim x4 -> x0, local copies, waits for them, and re-layouts: 11.5 us -> none  [pq_lookup(): lax.map(one_group, queries.reshape(count // size, size, queries.shape[1]))]
    convert_element_type x5 -> x0, local copies, waits for them, and re-layouts: 10.4 us -> none  [the longest x4 10.2 us: one_group(): return lookup.astype(jnp.bfloat16).reshape(size, subspaces * centroids)]
where the time goes in v1:
time: 49.1 us; the launch traced here: 48.9 us
  Pallas kernels  45.9 us (93%)
  local copies, waits for them, and re-layouts  2.39 us (5%)
  between operations  0.64 us (1%)
    pallas_call x1, Pallas kernels, per_device(): pl.pallas_call(lambda *refs: kernel_body(sizes, *refs), out_shape=(jax.Sh...  45.9 us
    unnamed x2, local copies, waits for them, and re-layouts  2.39 us

profile of v1, /device:TPU:1, one launch (start us, length us, event | category | flops | bytes accessed | tf_op | source)
XLA Modules:
  0.0 48.9 jit_solution(16551069576992838190)
XLA Ops:
  0.6 45.9 %recall.1 = (f32[3,4]{1,0:T(4,128)}, f32[1,3]{1,0:T(1,128)}) custom-call(s32[4]{0:T(128)} %refs_0_.1, bf16[4,1024]{1,0:T(4,128)(2,1)} %refs_1_.1, bf16[1024,1024]{1,0:T(8,128)(2,1)} %refs_2_.1, s32[64,1024]{1,0:T(8,128)} %bitcast.4, f32[64,16,256]{2,1,0:T(8,128)} %bitcast.3), custom_call_target="tpu_custom_call" | custom-call | tf_op jit(solution)/shard_map/recall/pallas_call | solution.py:263
  46.5 1.2 %copy.9 = f32[3,4]{1,0:T(4,128)} copy(f32[3,4]{1,0:T(4,128)} %get-tuple-element.8) | data formatting | bytes 96
  47.7 1.1 %copy.10 = f32[3]{0:T(128)} copy(f32[3]{0:T(128)} %bitcast.5) | data formatting | bytes 24

commit v2 on v1

--- a/solution.py
+++ b/solution.py
@@ -9,6 +9,22 @@
 SHARP = 50.0
 LANES = 128
 MESH = pl.DeviceIdType.MESH
+NX, NY, NZ = 2, 4, 8
+
+
+def distance(dx, dy, dz):
+    return dx + min(dy, NY - dy) + min(dz, NZ - dz)
+
+
+OFFSETS = sorted(
+    ((dx, dy, dz) for dx in range(NX) for dy in range(NY) for dz in range(NZ) if dx + dy + dz),
+    key=lambda offset: -distance(*offset),
+)
+FIRST = sorted(
+    ((dx, dz) for dx in range(NX) for dz in range(NZ) if dx + dz),
+    key=lambda offset: distance(offset[0], 0, offset[1]),
+)
+PLAN = ((16, FIRST[:4]), (24, FIRST[4:8]), (32, FIRST[8:12]), (40, FIRST[12:]), (64, ()))
 
 
 def kernel_body(
@@ -18,8 +34,8 @@
     residual_ref,
     codes_ref,
     codebook_ref,
-    hits_ref,
-    totals_ref,
+    result_ref,
+    own_queries,
     message,
     arrived,
     table,
@@ -39,7 +55,8 @@
     group_sums,
     local_sems,
     query_send,
-    query_recv,
+    near_recv,
+    far_recv,
     hit_send,
     hit_recv,
     total_send,
@@ -51,6 +68,7 @@
     my_pb = lax.axis_index("pb")
 
     loads = [
+        pltpu.make_async_copy(queries_ref, own_queries, local_sems.at[3]),
         pltpu.make_async_copy(codebook_ref, table, local_sems.at[0]),
         pltpu.make_async_copy(codes_ref, codes, local_sems.at[1]),
         pltpu.make_async_copy(residual_ref, residual, local_sems.at[2]),
@@ -58,52 +76,67 @@
     for load in loads:
         load.start()
 
+    my_x, my_y, my_z = lax.div(me, NY * NZ), lax.rem(lax.div(me, NZ), NY), lax.rem(me, NZ)
+
+    def ahead(dx, dy, dz):
+        x, y, z = lax.rem(my_x + dx, NX), lax.rem(my_y + dy, NY), lax.rem(my_z + dz, NZ)
+        return {"db": (x * NY + y) * NZ + z}
+
+    def behind(dx, dy, dz):
+        return ahead(NX - dx, NY - dy, NZ - dz)
+
     barrier = pltpu.get_barrier_semaphore()
-
-    def greet(step, _):
-        peer = lax.rem(me + step, db)
-        pl.semaphore_signal(barrier, inc=1, device_id={"db": peer}, device_id_type=MESH)
-        return 0
-
-    lax.fori_loop(1, db, greet, 0)
+    for dx, dy, dz in OFFSETS:
+        pl.semaphore_signal(barrier, inc=1, device_id=ahead(dx, dy, dz), device_id_type=MESH)
     for step in range(1, pb):
         peer = lax.rem(my_pb + step, pb)
         pl.semaphore_signal(barrier, inc=1, device_id={"pb": peer}, device_id_type=MESH)
 
-    message[:, :width] = queries_ref[...]
     row_ids = lax.broadcasted_iota(jnp.int32, (count, LANES), 0)
     rank_block = jnp.zeros((count, LANES), jnp.float32)
     for row in range(count):
         rank_block = jnp.where(row_ids == row, ranks_ref[row].astype(jnp.float32), rank_block)
     message[:, width:] = rank_block.astype(jnp.bfloat16)
+    loads[0].wait()
+    message[:, :width] = own_queries[...]
     arrived[0] = message[...]
-
-    pl.semaphore_wait(barrier, db - 1 + pb - 1)
-
-    def send_queries(step, _):
-        peer = lax.rem(me + step, db)
+    vector_bias[...] = jnp.zeros_like(vector_bias)
+    recon_bias[...] = jnp.zeros_like(recon_bias)
+
+    with jax.named_scope("wait_barrier"):
+        pl.semaphore_wait(barrier, db - 1 + pb - 1)
+
+    def forward(source, slot):
+        for dy in (2, 1, 3):
+            pltpu.make_async_remote_copy(
+                src_ref=source,
+                dst_ref=arrived.at[dy * NX * NZ + slot],
+                send_sem=query_send,
+                recv_sem=far_recv,
+                device_id=ahead(0, dy, 0),
+                device_id_type=MESH,
+            ).start()
+
+    for dx, dz in FIRST:
+        slot = dx * NZ + dz
         pltpu.make_async_remote_copy(
             src_ref=message,
-            dst_ref=arrived.at[step],
+            dst_ref=arrived.at[slot],
             send_sem=query_send,
-            recv_sem=query_recv,
-            device_id={"db": peer},
+            recv_sem=near_recv.at[slot],
+            device_id=ahead(dx, 0, dz),
             device_id_type=MESH,
         ).start()
-        return 0
-
-    lax.fori_loop(1, db, send_queries, 0)
-
-    for load in loads:
-        load.wait()
+    forward(message, 0)
 
     group = LANES // subdim
+    parts = width // LANES
 
     def prepare(index, _):
-        at, part = index // (width // LANES), lax.rem(index, width // LANES)
+        at, part = lax.div(index, parts), lax.rem(index, parts)
         n_at = pl.multiple_of(at * LANES, LANES)
         d_at = pl.multiple_of(part * LANES, LANES)
-        extra = residual[pl.ds(n_at, LANES), pl.ds(d_at, LANES)].astype(jnp.float32).T
+        extra = residual[pl.ds(n_at, LANES), pl.ds(d_at, LANES)].T
         chosen = codes[pl.ds(pl.multiple_of(part * group, group), group), pl.ds(n_at, LANES)]
         vector_norm = jnp.zeros((8, LANES), jnp.float32)
         recon_norm = jnp.zeros((8, LANES), jnp.float32)
@@ -118,7 +151,8 @@
                 entries[:, LANES:], low_pick, axis=1, mode="promise_in_bounds"
             )
             recon = jnp.where(pick >= LANES, above, below)
-            vector = (recon + extra[inner * subdim : (inner + 1) * subdim, :]).astype(jnp.bfloat16)
+            addend = extra[inner * subdim : (inner + 1) * subdim, :].astype(jnp.float32)
+            vector = (recon + addend).astype(jnp.bfloat16)
             high = recon.astype(jnp.bfloat16)
             low = (recon - high.astype(jnp.float32)).astype(jnp.bfloat16)
             here = pl.ds(pl.multiple_of(d_at + inner * subdim, subdim), subdim)
@@ -130,17 +164,25 @@
             vector_norm += squares[:8] + squares[8:]
             squares = recon * recon
             recon_norm += squares[:8] + squares[8:]
-
-        @pl.when(part == 0)
-        def _():
-            vector_bias[:, pl.ds(n_at, LANES)] = jnp.zeros((8, LANES), jnp.float32)
-            recon_bias[:, pl.ds(n_at, LANES)] = jnp.zeros((8, LANES), jnp.float32)
-
         vector_bias[:, pl.ds(n_at, LANES)] += vector_norm
         recon_bias[:, pl.ds(n_at, LANES)] += recon_norm
         return 0
 
-    lax.fori_loop(0, (rows // LANES) * (width // LANES), prepare, 0)
+    for load in loads[1:]:
+        load.wait()
+
+    done = 0
+    for upto, relays in PLAN:
+        if upto > done:
+            with jax.named_scope("prepare"):
+                lax.fori_loop(done, upto, prepare, 0, unroll=2)
+            done = upto
+        with jax.named_scope("relay"):
+            for dx, dz in relays:
+                slot = dx * NZ + dz
+                block = arrived.at[slot]
+                pltpu.make_async_copy(block, block, near_recv.at[slot]).wait()
+                forward(block, slot)
 
     scale = SHARP / 2
     vector_row = jnp.sum(vector_bias[...], axis=0, keepdims=True) * (-scale / width)
@@ -148,23 +190,25 @@
     vector_bias[...] = jnp.broadcast_to(vector_row, vector_bias.shape)
     recon_bias[...] = jnp.broadcast_to(recon_row, recon_bias.shape)
 
-    incoming = arrived.at[pl.ds(1, db - 1)]
-    pltpu.make_async_copy(incoming, incoming, query_recv).wait()
+    incoming = arrived.at[pl.ds(NX * NZ, db - NX * NZ)]
+    with jax.named_scope("wait_queries"):
+        pltpu.make_async_copy(incoming, incoming, far_recv).wait()
 
     stack = 16 // count
-
-    def unpack(index, _):
-        blocks = [arrived[index * stack + i].astype(jnp.float32) for i in range(stack)]
-        block = jnp.concatenate(blocks, axis=0)
-        here = pl.ds(pl.multiple_of(index * 16, 16), 16)
-        own = block[:, :width]
-        visiting[here, :] = own.astype(jnp.bfloat16)
-        norm = jnp.sum(own * own, axis=1, keepdims=True)
-        bound = 1.9 + 0.6 * block[:, width:] / (LEVELS - 1)
-        query_bias[here, :] = scale * bound - (scale / width) * norm
-        return 0
-
-    lax.fori_loop(0, db // stack, unpack, 0)
+    with jax.named_scope("unpack"):
+        for index in range(db // stack):
+            blocks = [arrived[index * stack + i].astype(jnp.float32) for i in range(stack)]
+            block = jnp.concatenate(blocks, axis=0)
+            here = slice(index * 16, index * 16 + 16)
+            own = block[:, :width]
+            visiting[here, :] = own.astype(jnp.bfloat16)
+            squares = own * own
+            folded = squares[:, :LANES]
+            for at in range(LANES, width, LANES):
+                folded += squares[:, at : at + LANES]
+            norm = jnp.sum(folded, axis=1, keepdims=True)
+            bound = 1.9 + 0.6 * block[:, width:] / (LEVELS - 1)
+            query_bias[here, :] = scale * bound - (scale / width) * norm
 
     total = db * count
     sums[...] = jnp.zeros_like(sums)
@@ -189,7 +233,8 @@
             sums[2] += exact_hit * coarse_hit
         return 0
 
-    lax.fori_loop(0, rows // tile, absorb, 0)
+    with jax.named_scope("absorb"):
+        lax.fori_loop(0, rows // tile, absorb, 0)
 
     lane = lax.broadcasted_iota(jnp.int32, (total, LANES), 1)
     place = lax.rem(lax.broadcasted_iota(jnp.int32, (total, LANES), 0), count)
@@ -211,21 +256,19 @@
     leaving[...] = folded.reshape(db, 1, LANES)
     returned[0] = folded[0:1, :]
 
-    def send_hits(step, _):
-        peer = lax.rem(me + db - step, db)
+    for dx, dy, dz in OFFSETS:
+        slot = (dy * NX + dx) * NZ + dz
         pltpu.make_async_remote_copy(
-            src_ref=leaving.at[step],
-            dst_ref=returned.at[step],
+            src_ref=leaving.at[slot],
+            dst_ref=returned.at[slot],
             send_sem=hit_send,
             recv_sem=hit_recv,
-            device_id={"db": peer},
+            device_id=behind(dx, dy, dz),
             device_id_type=MESH,
         ).start()
-        return 0
-
-    lax.fori_loop(1, db, send_hits, 0)
     landing = returned.at[pl.ds(1, db - 1)]
-    pltpu.make_async_copy(landing, landing, hit_recv).wait()
+    with jax.named_scope("wait_hits"):
+        pltpu.make_async_copy(landing, landing, hit_recv).wait()
     mine = jnp.sum(returned[...], axis=0)
     own_sums[...] = mine
     for step in range(1, pb):
@@ -237,15 +280,23 @@
             device_id={"pb": lax.rem(my_pb + step, pb)},
             device_id_type=MESH,
         ).start()
-    for kind in range(3):
-        hits_ref[kind : kind + 1, :] = mine[:, kind * count : (kind + 1) * count] * (1.0 / database)
-    pltpu.make_async_copy(group_sums, group_sums, total_recv).wait()
+    with jax.named_scope("wait_totals"):
+        pltpu.make_async_copy(group_sums, group_sums, total_recv).wait()
     all_sums = mine + jnp.sum(group_sums[...], axis=0)
-    totals_ref[...] = all_sums[:, 3 * count : 3 * count + 3] * (1.0 / (database * everyone))
-
-    pltpu.make_async_copy(incoming, incoming, query_send).wait()
+    result_ref[0:1, :] = mine * (1.0 / database)
+    result_ref[1:2, :] = all_sums * (1.0 / (database * everyone))
+
+    sent = arrived.at[pl.ds(1, db - 1)]
+    pltpu.make_async_copy(sent, sent, query_send).wait()
     pltpu.make_async_copy(landing, landing, hit_send).wait()
     pltpu.make_async_copy(group_sums, group_sums, total_send).wait()
+
+
+def place_outputs(result_ref, hits_ref, totals_ref):
+    count = hits_ref.shape[1]
+    for kind in range(3):
+        hits_ref[kind : kind + 1, :] = result_ref[0:1, kind * count : (kind + 1) * count]
+    totals_ref[...] = result_ref[1:2, 3 * count : 3 * count + 3]
 
 
 def solution(mesh):
@@ -260,21 +311,13 @@
         in_vmem = pl.BlockSpec(memory_space=pltpu.VMEM)
         anywhere = pl.BlockSpec(memory_space=pl.ANY)
         dma = pltpu.SemaphoreType.DMA
-        hits, totals = pl.pallas_call(
+        result = pl.pallas_call(
             lambda *refs: kernel_body(sizes, *refs),
-            out_shape=(
-                jax.ShapeDtypeStruct((3, count), jnp.float32),
-                jax.ShapeDtypeStruct((1, 3), jnp.float32),
-            ),
-            in_specs=[
-                pl.BlockSpec(memory_space=pltpu.SMEM),
-                in_vmem,
-                anywhere,
-                anywhere,
-                anywhere,
-            ],
-            out_specs=(in_vmem, in_vmem),
+            out_shape=jax.ShapeDtypeStruct((8, LANES), jnp.float32),
+            in_specs=[pl.BlockSpec(memory_space=pltpu.SMEM)] + [anywhere] * 4,
+            out_specs=in_vmem,
             scratch_shapes=[
+                pltpu.VMEM((count, width), jnp.bfloat16),
                 pltpu.VMEM((count, width + LANES), jnp.bfloat16),
                 pltpu.VMEM((db, count, width + LANES), jnp.bfloat16),
                 pltpu.VMEM((subspaces, subdim, centroids), jnp.float32),
@@ -292,8 +335,9 @@
                 pltpu.VMEM((db, 1, LANES), jnp.float32),
                 pltpu.VMEM((1, LANES), jnp.float32),
                 pltpu.VMEM((pb - 1, 1, LANES), jnp.float32),
-                dma((3,)),
-                dma,
+                dma((4,)),
+                dma,
+                dma((NX * NZ,)),
                 dma,
                 dma,
                 dma,
@@ -305,6 +349,14 @@
             ),
             name="recall",
         )(ranks, queries, residual, codes.T, jnp.transpose(codebook, (0, 2, 1)))
+        hits, totals = pl.pallas_call(
+            place_outputs,
+            out_shape=(
+                jax.ShapeDtypeStruct((3, count), jnp.float32),
+                jax.ShapeDtypeStruct((1, 3), jnp.float32),
+            ),
+            name="place",
+        )(result)
         return hits, totals.reshape(3)
 
     return jax.shard_map(

time: 49.1 us -> 39.8 us (0.81)
  Pallas kernels: 45.9 us -> 39 us
  local copies, waits for them, and re-layouts: 2.39 us -> 0 us
    pallas_call x1 -> x2, Pallas kernels: 45.9 us -> 39 us  [the longest x1 37.7 us: per_device(): pl.pallas_call(lambda *refs: kernel_body(sizes, *refs), out_shape=jax.Sha...]
    unnamed x2 -> x0, local copies, waits for them, and re-layouts: 2.39 us -> none
where the time goes in v2:
time: 39.8 us; the launch traced here: 39.7 us
  Pallas kernels  39 us (98%)
  between operations  0.64 us (2%)
    pallas_call x1, Pallas kernels, per_device(): pl.pallas_call(lambda *refs: kernel_body(sizes, *refs), out_shape=jax.Sha...  37.7 us
    pallas_call x1, Pallas kernels, per_device(): pl.pallas_call(place_outputs, out_shape=(jax.ShapeDtypeStruct((3, count),...  1.32 us

profile of v2, /device:TPU:1, one launch (start us, length us, event | category | flops | bytes accessed | tf_op | source)
XLA Modules:
  0.0 39.7 jit_solution(16153384548662137130)
XLA Ops:
  0.6 37.7 %recall.1.result_ref = f32[8,128]{1,0:T(8,128)} custom-call(s32[4]{0:T(128)} %refs_0_.1, bf16[4,1024]{1,0:T(4,128)(2,1)} %refs_1_.1, bf16[1024,1024]{1,0:T(8,128)(2,1)} %refs_2_.1, s32[64,1024]{1,0:T(8,128)} %bitcast.4, f32[64,16,256]{2,1,0:T(8,128)} %bitcast.3), custom_call_target="tpu_custom_call" | custom-call | tf_op jit(solution)/shard_map/recall/pallas_call | solution.py:314
  38.3 1.3 %place.1 = (f32[3,4]{1,0:T(4,128)}, f32[1,3]{1,0:T(1,128)}) custom-call(f32[8,128]{1,0:T(8,128)} %recall.1.result_ref), custom_call_target="tpu_custom_call" | custom-call | tf_op jit(solution)/shard_map/place/pallas_call | solution.py:352

commit v3 on v2

v3 whole, which is shorter than its diff:
```python
import jax
import jax.numpy as jnp
from jax import lax
from jax.experimental import pallas as pl
from jax.experimental.pallas import tpu as pltpu
from jax.sharding import PartitionSpec as P

LEVELS = 64
SCALE = 25.0
LANES = 128
MESH = pl.DeviceIdType.MESH
NX, NY, NZ = 2, 4, 8
PLANE = NX * NZ


def ring(step, length):
    return min(step, length - step)


def near_first(steps):
    return sorted(steps, key=lambda step: ring(step[0], NX) + ring(step[1], NZ))


FIRST = near_first([(dx, dz) for dx in range(NX) for dz in range(NZ) if dx + dz])
ACROSS = sorted(
    ((dy, dz) for dy in range(NY) for dz in range(NZ) if dy + dz),
    key=lambda step: -ring(step[0], NY) - ring(step[1], NZ),
)
PLAN = ((16, FIRST[:4]), (24, FIRST[4:8]), (32, FIRST[8:12]), (40, FIRST[12:]), (64, ()))


def start_copy(source, target, send_sem, recv_sem, device):
    pltpu.make_async_remote_copy(
        src_ref=source,
        dst_ref=target,
        send_sem=send_sem,
        recv_sem=recv_sem,
        device_id=device,
        device_id_type=MESH,
    ).start()


def wait_bytes(block, sem):
    pltpu.make_async_copy(block, block, sem).wait()


def kernel_body(
    sizes,
    ranks_ref,
    queries_ref,
    residual_ref,
    codes_ref,
    codebook_ref,
    result_ref,
    own_ranks,
    own_queries,
    message,
    arrived,
    table,
    codes,
    residual,
    vectors,
    recons,
    vector_bias,
    recon_bias,
    visiting,
    query_bias,
    sums,
    leaving,
    returned,
    own_sums,
    side_sums,
    local_sems,
    query_send,
    near_recv,
    far_recv,
    hit_send,
    hit_recv,
    side_send,
    side_recv,
):
    db, pb, rows, width, database, everyone, subdim = sizes
    count = own_queries.shape[0]
    me = lax.axis_index("db")
    my_pb = lax.axis_index("pb")

    loads = [
        pltpu.make_async_copy(ranks_ref, own_ranks, local_sems.at[4]),
        pltpu.make_async_copy(queries_ref, own_queries, local_sems.at[3]),
        pltpu.make_async_copy(codebook_ref, table, local_sems.at[0]),
        pltpu.make_async_copy(codes_ref, codes, local_sems.at[1]),
        pltpu.make_async_copy(residual_ref, residual, local_sems.at[2]),
    ]
    for load in loads:
        load.start()

    my_x, my_y, my_z = lax.div(me, NY * NZ), lax.rem(lax.div(me, NZ), NY), lax.rem(me, NZ)

    def ahead(dx, dy, dz):
        x, y, z = lax.rem(my_x + dx, NX), lax.rem(my_y + dy, NY), lax.rem(my_z + dz, NZ)
        return (x * NY + y) * NZ + z

    def beside(dp, dx):
        return {"pb": lax.rem(my_pb + dp, pb), "db": ahead(dx, 0, 0)}

    sides = [(dp, dx) for dp in range(pb) for dx in range(NX) if dp + dx]

    barrier = pltpu.get_barrier_semaphore()
    greeted = [{"db": ahead(dx, 0, dz)} for dx, dz in FIRST[::-1]]
    greeted += [{"db": ahead(0, dy, 0)} for dy in range(1, NY)]
    greeted += [beside(dp, dx) for dp, dx in sides if dp]
    for device in greeted:
        pl.semaphore_signal(barrier, inc=1, device_id=device, device_id_type=MESH)

    row_ids = lax.broadcasted_iota(jnp.int32, (count, LANES), 0)
    rank_block = jnp.zeros((count, LANES), jnp.float32)
    loads[0].wait()
    for row in range(count):
        rank_block = jnp.where(row_ids == row, own_ranks[row].astype(jnp.float32), rank_block)
    message[:, width:] = rank_block.astype(jnp.bfloat16)
    loads[1].wait()
    message[:, :width] = own_queries[...]
    arrived[0] = message[...]
    vector_bias[...] = jnp.zeros_like(vector_bias)
    recon_bias[...] = jnp.zeros_like(recon_bias)

    with jax.named_scope("wait_barrier"):
        pl.semaphore_wait(barrier, len(greeted))

    def forward(source, slot):
        for dy in (2, 1, 3):
            start_copy(
                source,
                arrived.at[dy * PLANE + slot],
                query_send,
                far_recv.at[dy],
                {"db": ahead(0, dy, 0)},
            )

    for dx, dz in FIRST:
        slot = dx * NZ + dz
        start_copy(
            message, arrived.at[slot], query_send, near_recv.at[slot], {"db": ahead(dx, 0, dz)}
        )
    forward(message, 0)

    group = LANES // subdim
    parts = width // LANES

    def prepare(index, _):
        at, part = lax.div(index, parts), lax.rem(index, parts)
        n_at = pl.multiple_of(at * LANES, LANES)
        d_at = pl.multiple_of(part * LANES, LANES)
        extra = residual[pl.ds(n_at, LANES), pl.ds(d_at, LANES)].T
        chosen = codes[pl.ds(pl.multiple_of(part * group, group), group), pl.ds(n_at, LANES)]
        vector_norm = jnp.zeros((8, LANES), jnp.float32)
        recon_norm = jnp.zeros((8, LANES), jnp.float32)
        for inner in range(group):
            pick = jnp.broadcast_to(chosen[inner : inner + 1, :], (subdim, LANES))
            low_pick = pick & (LANES - 1)
            entries = table[part * group + inner]
            below = jnp.take_along_axis(
                entries[:, :LANES], low_pick, axis=1, mode="promise_in_bounds"
            )
            above = jnp.take_along_axis(
                entries[:, LANES:], low_pick, axis=1, mode="promise_in_bounds"
            )
            recon = jnp.where(pick >= LANES, above, below)
            addend = extra[inner * subdim : (inner + 1) * subdim, :].astype(jnp.float32)
            vector = (recon + addend).astype(jnp.bfloat16)
            here = pl.ds(pl.multiple_of(d_at + inner * subdim, subdim), subdim)
            vectors[here, pl.ds(n_at, LANES)] = vector
            recons[here, pl.ds(n_at, LANES)] = recon.astype(jnp.bfloat16)
            wide = vector.astype(jnp.float32)
            squares = wide * wide
            vector_norm += squares[:8] + squares[8:]
            squares = recon * recon
            recon_norm += squares[:8] + squares[8:]
        vector_bias[:, pl.ds(n_at, LANES)] += vector_norm
        recon_bias[:, pl.ds(n_at, LANES)] += recon_norm
        return 0

    for load in loads[2:]:
        load.wait()

    done = 0
    for upto, relays in PLAN:
        if upto > done:
            with jax.named_scope("prepare"):
                lax.fori_loop(done, upto, prepare, 0, unroll=UNROLL)
            done = upto
        with jax.named_scope("relay"):
            for dx, dz in relays:
                slot = dx * NZ + dz
                block = arrived.at[slot]
                wait_bytes(block, near_recv.at[slot])
                forward(block, slot)

    vector_row = jnp.sum(vector_bias[...], axis=0, keepdims=True) * (-SCALE / width)
    recon_row = jnp.sum(recon_bias[...], axis=0, keepdims=True) * (-SCALE / width)
    vector_bias[...] = jnp.broadcast_to(vector_row, vector_bias.shape)
    recon_bias[...] = jnp.broadcast_to(recon_row, recon_bias.shape)

    stack = 16 // count
    tile = 256
    half = 2 * PLANE * count
    sums[...] = jnp.zeros_like(sums)

    def unpack(first, last):
        for index in range(first // stack, last // stack):
            blocks = [arrived[index * stack + i].astype(jnp.float32) for i in range(stack)]
            block = jnp.concatenate(blocks, axis=0)
            here = slice(index * 16, index * 16 + 16)
            own = block[:, :width]
            visiting[here, :] = own.astype(jnp.bfloat16)
            squares = own * own
            folded = squares[:, :LANES]
            for at in range(LANES, width, LANES):
                folded += squares[:, at : at + LANES]
            norm = jnp.sum(folded, axis=1, keepdims=True)
            bound = 1.9 + 0.6 * block[:, width:] / (LEVELS - 1)
            query_bias[here, :] = SCALE * bound - (SCALE / width) * norm

    def absorb(first):
        q_at = slice(first, first + half)

        def one(index, _):
            n_at = pl.ds(pl.multiple_of(index * tile, tile), tile)
            mine = visiting[q_at, :]
            cross = jnp.dot(mine, vectors[:, n_at], preferred_element_type=jnp.float32)
            coarse_cross = jnp.dot(mine, recons[:, n_at], preferred_element_type=jnp.float32)
            bias = query_bias[q_at, :]
            parts = [0.0, 0.0, 0.0]
            for at in range(0, tile, LANES):
                row_at = pl.ds(pl.multiple_of(index * tile + at, LANES), LANES)
                lanes = slice(at, at + LANES)
                exact = bias + (vector_bias[0:1, row_at] + cross[:, lanes] * (2 * SCALE / width))
                coarse = bias + (recon_bias[0:1, row_at] + coarse_cross[:, lanes] * (2 * SCALE / width))
                exact_hit = 1.0 + jnp.tanh(exact)
                coarse_hit = 1.0 + jnp.tanh(coarse)
                parts[0] += exact_hit
                parts[1] += coarse_hit
                parts[2] += exact_hit * coarse_hit
            for kind in range(3):
                sums[kind, q_at, :] += parts[kind]
            return 0

        lax.fori_loop(0, rows // tile, one, 0, unroll=ABSORB_UNROLL)

    def plane(dy):
        return arrived.at[pl.ds(dy * PLANE, PLANE)]

    with jax.named_scope("wait_queries1"):
        wait_bytes(plane(1), far_recv.at[1])
    with jax.named_scope("unpack"):
        unpack(0, 2 * PLANE)
    with jax.named_scope("absorb"):
        absorb(0)
    with jax.named_scope("wait_queries2"):
        wait_bytes(plane(3), far_recv.at[3])
        wait_bytes(plane(2), far_recv.at[2])
    with jax.named_scope("unpack"):
        unpack(2 * PLANE, db)
    with jax.named_scope("absorb"):
        absorb(half)

    total = db * count
    lane = lax.broadcasted_iota(jnp.int32, (total, LANES), 1)
    row = lax.broadcasted_iota(jnp.int32, (total, LANES), 0)
    side_x = lax.rem(lax.div(row, NZ * count), NX)
    base = 16 * side_x + lax.rem(row, count)
    spread = jnp.zeros((total, LANES), jnp.float32)
    for kind in range(3):
        weight = 0.25 if kind == 2 else 0.5
        column = jnp.sum(sums[kind], axis=1, keepdims=True) * weight
        spread = jnp.where(lane == base + count * kind, column, spread)
        spread = jnp.where(lane == 64 + kind, column, spread)
    out_row = lax.broadcasted_iota(jnp.int32, (NY * NZ, total), 0)
    from_row = lax.broadcasted_iota(jnp.int32, (NY * NZ, total), 1)
    from_slot = lax.div(from_row, count)
    from_place = lax.div(from_slot, PLANE) * NZ + lax.rem(from_slot, NZ)
    folder = (from_place == out_row).astype(jnp.float32)
    folded = jnp.dot(
        folder, spread, preferred_element_type=jnp.float32, precision=lax.Precision.HIGHEST
    )
    overall = jnp.sum(spread, axis=0, keepdims=True)
    short_lane = lax.broadcasted_iota(jnp.int32, (NY * NZ, LANES), 1)
    folded = jnp.where(short_lane < 64, folded, overall)
    leaving[...] = folded.reshape(NY * NZ, 1, LANES)
    returned[0] = folded[0:1, :]

    for dy, dz in ACROSS:
        place = dy * NZ + dz
        start_copy(
            leaving.at[place],
            returned.at[place],
            hit_send,
            hit_recv,
            {"db": ahead(0, NY - dy, NZ - dz)},
        )
    landing = returned.at[pl.ds(1, NY * NZ - 1)]
    with jax.named_scope("wait_hits"):
        wait_bytes(landing, hit_recv)
    mine = jnp.sum(returned[...], axis=0)
    own_sums[...] = mine
    for place, (dp, dx) in enumerate(sides):
        start_copy(own_sums, side_sums.at[place], side_send, side_recv, beside(dp, dx))
    with jax.named_scope("wait_totals"):
        wait_bytes(side_sums, side_recv)
    all_sums = mine + jnp.sum(side_sums[...], axis=0)
    partner = side_sums[sides.index((0, 1))]
    result_ref[0:1, :] = mine * (1.0 / database)
    result_ref[1:2, :] = partner * (1.0 / database)
    result_ref[2:3, :] = all_sums * (1.0 / (database * everyone))

    sent = arrived.at[pl.ds(1, db - 1)]
    wait_bytes(sent, query_send)
    wait_bytes(landing, hit_send)
    wait_bytes(side_sums, side_send)


UNROLL = 4
ABSORB_UNROLL = 2


def place_outputs(result_ref, hits_ref, totals_ref):
    count = hits_ref.shape[1]
    for kind in range(3):
        first = result_ref[0:1, kind * count : (kind + 1) * count]
        second = result_ref[1:2, 16 + kind * count : 16 + (kind + 1) * count]
        hits_ref[kind : kind + 1, :] = first + second
    totals_ref[...] = result_ref[2:3, 64:67]


def solution(mesh):
    db, pb = mesh.shape["db"], mesh.shape["pb"]

    def per_device(queries, residual, codes, codebook, ranks):
        count, width = queries.shape
        rows = residual.shape[0]
        subspaces, centroids, subdim = codebook.shape
        sizes = (db, pb, rows, width, rows * db, count * pb * db, subdim)
        total = db * count
        in_vmem = pl.BlockSpec(memory_space=pltpu.VMEM)
        anywhere = pl.BlockSpec(memory_space=pl.ANY)
        dma = pltpu.SemaphoreType.DMA
        result = pl.pallas_call(
            lambda *refs: kernel_body(sizes, *refs),
            out_shape=pltpu.VMEM((8, LANES), jnp.float32),
            in_specs=[anywhere] * 5,
            out_specs=in_vmem,
            scratch_shapes=[
                pltpu.SMEM((count,), jnp.int32),
                pltpu.VMEM((count, width), jnp.bfloat16),
                pltpu.VMEM((count, width + LANES), jnp.bfloat16),
                pltpu.VMEM((db, count, width + LANES), jnp.bfloat16),
                pltpu.VMEM((subspaces, subdim, centroids), jnp.float32),
                pltpu.VMEM((subspaces, rows), jnp.int32),
                pltpu.VMEM((rows, width), jnp.bfloat16),
                pltpu.VMEM((width, rows), jnp.bfloat16),
                pltpu.VMEM((width, rows), jnp.bfloat16),
                pltpu.VMEM((8, rows), jnp.float32),
                pltpu.VMEM((8, rows), jnp.float32),
                pltpu.VMEM((total, width), jnp.bfloat16),
                pltpu.VMEM((total, LANES), jnp.float32),
                pltpu.VMEM((3, total, LANES), jnp.float32),
                pltpu.VMEM((NY * NZ, 1, LANES), jnp.float32),
                pltpu.VMEM((NY * NZ, 1, LANES), jnp.float32),
                pltpu.VMEM((1, LANES), jnp.float32),
                pltpu.VMEM((pb * NX - 1, 1, LANES), jnp.float32),
                dma((5,)),
                dma,
                dma((PLANE,)),
                dma((NY,)),
                dma,
                dma,
                dma,
                dma,
            ],
            compiler_params=pltpu.CompilerParams(
                collective_id=0, has_side_effects=True, vmem_limit_bytes=60 * 1024 * 1024
            ),
            name="recall",
        )(ranks, queries, residual, codes.T, jnp.transpose(codebook, (0, 2, 1)))
        hits, totals = pl.pallas_call(
            place_outputs,
            out_shape=(
                jax.ShapeDtypeStruct((3, count), jnp.float32),
                jax.ShapeDtypeStruct((1, 3), jnp.float32),
            ),
            in_specs=[in_vmem],
            name="place",
        )(pltpu.with_memory_space_constraint(result, pltpu.VMEM))
        return hits, totals.reshape(3)

    return jax.shard_map(
        per_device,
        mesh=mesh,
        in_specs=(P(("pb", "db"), None), P("db", None), P("db", None), P(), P(("pb", "db"))),
        out_specs=(P(None, ("pb", "db")), P()),
        check_vma=False,
    )
```

time: 39.8 us -> 35 us (0.88)
  Pallas kernels: 39 us -> 34.3 us
    pallas_call x1, Pallas kernels: 37.7 us -> 33.6 us  [per_device(): pl.pallas_call(lambda *refs: kernel_body(sizes, *refs), out_shape=pltpu.V...]
    pallas_call x1, Pallas kernels: 1.32 us -> 0.72 us  [per_device(): pl.pallas_call(place_outputs, out_shape=(jax.ShapeDtypeStruct((3, count),...]
where the time goes in v3:
time: 35 us; the launch traced here: 34.9 us
  Pallas kernels  34.3 us (98%)
  between operations  0.64 us (2%)
    pallas_call x1, Pallas kernels, per_device(): pl.pallas_call(lambda *refs: kernel_body(sizes, *refs), out_shape=pltpu.V...  33.6 us
    pallas_call x1, Pallas kernels, per_device(): pl.pallas_call(place_outputs, out_shape=(jax.ShapeDtypeStruct((3, count),...  0.72 us

profile of v3, /device:TPU:1, one launch (start us, length us, event | category | flops | bytes accessed | tf_op | source)
XLA Modules:
  0.0 34.9 jit_solution(2286714687667132267)
XLA Ops:
  0.6 33.6 %recall.1.result_ref = f32[8,128]{1,0:T(8,128)S(1)} custom-call(s32[4]{0:T(128)} %refs_0_.1, bf16[4,1024]{1,0:T(4,128)(2,1)} %refs_1_.1, bf16[1024,1024]{1,0:T(8,128)(2,1)} %refs_2_.1, s32[64,1024]{1,0:T(8,128)} %bitcast.4, f32[64,16,256]{2,1,0:T(8,128)} %bitcast.3), custom_call_target="tpu_custom_call" | custom-call | tf_op jit(solution)/shard_map/recall/pallas_call | solution.py:347
  34.2 0.7 %place.1 = (f32[3,4]{1,0:T(4,128)}, f32[1,3]{1,0:T(1,128)}) custom-call(f32[8,128]{1,0:T(8,128)S(1)} %recall.1.result_ref), custom_call_target="tpu_custom_call" | custom-call | tf_op jit(solution)/shard_map/place/pallas_call | solution.py:385

commit v4 on v3

--- a/solution.py
+++ b/solution.py
@@ -10,23 +10,38 @@
 LANES = 128
 MESH = pl.DeviceIdType.MESH
 NX, NY, NZ = 2, 4, 8
-PLANE = NX * NZ
+PLANE = NX * NY
+FIRST_COLUMNS = 768
+Z_STEPS = (0, 1, 7, 2, 6, 3, 5, 4)
+XY_STEPS = ((0, 0), (0, 1), (0, 3), (1, 0), (1, 1), (1, 3), (0, 2), (1, 2))
 
 
 def ring(step, length):
     return min(step, length - step)
 
 
-def near_first(steps):
-    return sorted(steps, key=lambda step: ring(step[0], NX) + ring(step[1], NZ))
-
-
-FIRST = near_first([(dx, dz) for dx in range(NX) for dz in range(NZ) if dx + dz])
 ACROSS = sorted(
-    ((dy, dz) for dy in range(NY) for dz in range(NZ) if dy + dz),
-    key=lambda step: -ring(step[0], NY) - ring(step[1], NZ),
+    ((dy, at) for dy in range(NY) for at in range(NZ) if dy + at),
+    key=lambda step: -ring(step[0], NY) - ring(Z_STEPS[step[1]], NZ),
 )
-PLAN = ((16, FIRST[:4]), (24, FIRST[4:8]), (32, FIRST[8:12]), (40, FIRST[12:]), (64, ()))
+PLAN = ((16, (1, 2), (1, 2, 3)), (20, (3, 4), (4, 5, 6)), (24, (5, 6), (7,)), (28, (7,), ()), (64, (), ()))
+
+
+def lane_gather(rows, index):
+    numbers = lax.GatherDimensionNumbers(
+        offset_dims=(),
+        collapsed_slice_dims=(1,),
+        start_index_map=(1,),
+        operand_batching_dims=(0,),
+        start_indices_batching_dims=(0,),
+    )
+    return lax.gather(
+        rows,
+        index[:, :, None],
+        dimension_numbers=numbers,
+        slice_sizes=(1, 1),
+        mode=lax.GatherScatterMode.PROMISE_IN_BOUNDS,
+    )
 
 
 def start_copy(source, target, send_sem, recv_sem, device):
@@ -66,14 +81,18 @@
     visiting,
     query_bias,
     sums,
+    lane_place,
+    folder,
     leaving,
     returned,
     own_sums,
     side_sums,
     local_sems,
     query_send,
-    near_recv,
-    far_recv,
+    near_first,
+    near_second,
+    far_first,
+    far_second,
     hit_send,
     hit_recv,
     side_send,
@@ -106,8 +125,8 @@
     sides = [(dp, dx) for dp in range(pb) for dx in range(NX) if dp + dx]
 
     barrier = pltpu.get_barrier_semaphore()
-    greeted = [{"db": ahead(dx, 0, dz)} for dx, dz in FIRST[::-1]]
-    greeted += [{"db": ahead(0, dy, 0)} for dy in range(1, NY)]
+    greeted = [{"db": ahead(0, 0, dz)} for dz in Z_STEPS[:0:-1]]
+    greeted += [{"db": ahead(dx, dy, 0)} for dx, dy in XY_STEPS[:0:-1]]
     greeted += [beside(dp, dx) for dp, dx in sides if dp]
     for device in greeted:
         pl.semaphore_signal(barrier, inc=1, device_id=device, device_id_type=MESH)
@@ -127,22 +146,49 @@
     with jax.named_scope("wait_barrier"):
         pl.semaphore_wait(barrier, len(greeted))
 
-    def forward(source, slot):
-        for dy in (2, 1, 3):
+    first_part, second_part = pl.ds(0, FIRST_COLUMNS), pl.ds(FIRST_COLUMNS, width + LANES - FIRST_COLUMNS)
+    half_steps = NZ // 2
+
+    def send_xy(source, at):
+        for group_at in range(PLANE - 1, 0, -1):
+            dx, dy = XY_STEPS[group_at]
             start_copy(
                 source,
-                arrived.at[dy * PLANE + slot],
+                arrived.at[at * PLANE + group_at, :, first_part],
                 query_send,
-                far_recv.at[dy],
-                {"db": ahead(0, dy, 0)},
+                far_first.at[at // half_steps],
+                {"db": ahead(dx, dy, 0)},
             )
 
-    for dx, dz in FIRST:
-        slot = dx * NZ + dz
+    def send_z(source, group_at):
+        for at in range(NZ - 1, 0, -1):
+            start_copy(
+                source,
+                arrived.at[at * PLANE + group_at, :, second_part],
+                query_send,
+                far_second.at[at // half_steps],
+                {"db": ahead(0, 0, Z_STEPS[at])},
+            )
+
+    for at in range(1, NZ):
         start_copy(
-            message, arrived.at[slot], query_send, near_recv.at[slot], {"db": ahead(dx, 0, dz)}
+            message.at[:, first_part],
+            arrived.at[at * PLANE, :, first_part],
+            query_send,
+            near_first.at[at],
+            {"db": ahead(0, 0, Z_STEPS[at])},
         )
-    forward(message, 0)
+    for group_at in range(1, PLANE):
+        dx, dy = XY_STEPS[group_at]
+        start_copy(
+            message.at[:, second_part],
+            arrived.at[group_at, :, second_part],
+            query_send,
+            near_second.at[group_at],
+            {"db": ahead(dx, dy, 0)},
+        )
+    send_xy(message.at[:, first_part], 0)
+    send_z(message.at[:, second_part], 0)
 
     group = LANES // subdim
     parts = width // LANES
@@ -159,12 +205,8 @@
             pick = jnp.broadcast_to(chosen[inner : inner + 1, :], (subdim, LANES))
             low_pick = pick & (LANES - 1)
             entries = table[part * group + inner]
-            below = jnp.take_along_axis(
-                entries[:, :LANES], low_pick, axis=1, mode="promise_in_bounds"
-            )
-            above = jnp.take_along_axis(
-                entries[:, LANES:], low_pick, axis=1, mode="promise_in_bounds"
-            )
+            below = lane_gather(entries[:, :LANES], low_pick)
+            above = lane_gather(entries[:, LANES:], low_pick)
             recon = jnp.where(pick >= LANES, above, below)
             addend = extra[inner * subdim : (inner + 1) * subdim, :].astype(jnp.float32)
             vector = (recon + addend).astype(jnp.bfloat16)
@@ -184,17 +226,37 @@
         load.wait()
 
     done = 0
-    for upto, relays in PLAN:
-        if upto > done:
-            with jax.named_scope("prepare"):
-                lax.fori_loop(done, upto, prepare, 0, unroll=UNROLL)
-            done = upto
+    for upto, z_arrivals, xy_arrivals in PLAN:
+        with jax.named_scope("prepare"):
+            lax.fori_loop(done, upto, prepare, 0, unroll=UNROLL)
+        done = upto
         with jax.named_scope("relay"):
-            for dx, dz in relays:
-                slot = dx * NZ + dz
-                block = arrived.at[slot]
-                wait_bytes(block, near_recv.at[slot])
-                forward(block, slot)
+            for at in z_arrivals:
+                block = arrived.at[at * PLANE, :, first_part]
+                wait_bytes(block, near_first.at[at])
+                send_xy(block, at)
+            for group_at in xy_arrivals:
+                block = arrived.at[group_at, :, second_part]
+                wait_bytes(block, near_second.at[group_at])
+                send_z(block, group_at)
+
+    total = db * count
+    lane = lax.broadcasted_iota(jnp.int32, (total, LANES), 1)
+    row = lax.broadcasted_iota(jnp.int32, (total, LANES), 0)
+    row_group = lax.rem(lax.div(row, count), PLANE)
+    base = lax.rem(row, count)
+    for group_at, (dx, dy) in enumerate(XY_STEPS):
+        if dx:
+            base = jnp.where(row_group == group_at, base + 16, base)
+    lane_place[...] = lane - base
+    out_row = lax.broadcasted_iota(jnp.int32, (NY * NZ, total), 0)
+    from_row = lax.broadcasted_iota(jnp.int32, (NY * NZ, total), 1)
+    from_group = lax.rem(lax.div(from_row, count), PLANE)
+    from_place = lax.div(from_row, PLANE * count)
+    for group_at, (dx, dy) in enumerate(XY_STEPS):
+        if dy:
+            from_place = jnp.where(from_group == group_at, from_place + dy * NZ, from_place)
+    folder[...] = (from_place == out_row).astype(jnp.float32).astype(jnp.bfloat16)
 
     vector_row = jnp.sum(vector_bias[...], axis=0, keepdims=True) * (-SCALE / width)
     recon_row = jnp.sum(recon_bias[...], axis=0, keepdims=True) * (-SCALE / width)
@@ -203,7 +265,7 @@
 
     stack = 16 // count
     tile = 256
-    half = 2 * PLANE * count
+    half = half_steps * PLANE * count
     sums[...] = jnp.zeros_like(sums)
 
     def unpack(first, last):
@@ -247,56 +309,54 @@
 
         lax.fori_loop(0, rows // tile, one, 0, unroll=ABSORB_UNROLL)
 
-    def plane(dy):
-        return arrived.at[pl.ds(dy * PLANE, PLANE)]
+    def wait_half(which):
+        steps = half_steps - 1 + which
+        first_span = pl.ds(which * half_steps * PLANE + 1, half_steps * (PLANE - 1))
+        wait_bytes(arrived.at[first_span, :, first_part], far_first.at[which])
+        start = half_steps if which else 1
+        second_span = pl.ds(start * PLANE, steps * PLANE)
+        wait_bytes(arrived.at[second_span, :, second_part], far_second.at[which])
 
     with jax.named_scope("wait_queries1"):
-        wait_bytes(plane(1), far_recv.at[1])
+        wait_half(0)
     with jax.named_scope("unpack"):
-        unpack(0, 2 * PLANE)
+        unpack(0, half_steps * PLANE)
     with jax.named_scope("absorb"):
         absorb(0)
     with jax.named_scope("wait_queries2"):
-        wait_bytes(plane(3), far_recv.at[3])
-        wait_bytes(plane(2), far_recv.at[2])
+        wait_half(1)
     with jax.named_scope("unpack"):
-        unpack(2 * PLANE, db)
+        unpack(half_steps * PLANE, db)
     with jax.named_scope("absorb"):
         absorb(half)
 
-    total = db * count
-    lane = lax.broadcasted_iota(jnp.int32, (total, LANES), 1)
-    row = lax.broadcasted_iota(jnp.int32, (total, LANES), 0)
-    side_x = lax.rem(lax.div(row, NZ * count), NX)
-    base = 16 * side_x + lax.rem(row, count)
     spread = jnp.zeros((total, LANES), jnp.float32)
+    place = lane_place[...]
+    overall = []
     for kind in range(3):
         weight = 0.25 if kind == 2 else 0.5
         column = jnp.sum(sums[kind], axis=1, keepdims=True) * weight
-        spread = jnp.where(lane == base + count * kind, column, spread)
-        spread = jnp.where(lane == 64 + kind, column, spread)
-    out_row = lax.broadcasted_iota(jnp.int32, (NY * NZ, total), 0)
-    from_row = lax.broadcasted_iota(jnp.int32, (NY * NZ, total), 1)
-    from_slot = lax.div(from_row, count)
-    from_place = lax.div(from_slot, PLANE) * NZ + lax.rem(from_slot, NZ)
-    folder = (from_place == out_row).astype(jnp.float32)
-    folded = jnp.dot(
-        folder, spread, preferred_element_type=jnp.float32, precision=lax.Precision.HIGHEST
-    )
-    overall = jnp.sum(spread, axis=0, keepdims=True)
+        spread = jnp.where(place == count * kind, column, spread)
+        overall.append(jnp.sum(column, axis=0, keepdims=True))
+    rest, folded = spread, 0.0
+    for _ in range(3):
+        piece = rest.astype(jnp.bfloat16)
+        rest = rest - piece.astype(jnp.float32)
+        folded += jnp.dot(folder[...], piece, preferred_element_type=jnp.float32)
     short_lane = lax.broadcasted_iota(jnp.int32, (NY * NZ, LANES), 1)
-    folded = jnp.where(short_lane < 64, folded, overall)
+    for kind in range(3):
+        folded = jnp.where(short_lane == 64 + kind, overall[kind], folded)
     leaving[...] = folded.reshape(NY * NZ, 1, LANES)
     returned[0] = folded[0:1, :]
 
-    for dy, dz in ACROSS:
-        place = dy * NZ + dz
+    for dy, at in ACROSS:
+        place = dy * NZ + at
         start_copy(
             leaving.at[place],
             returned.at[place],
             hit_send,
             hit_recv,
-            {"db": ahead(0, NY - dy, NZ - dz)},
+            {"db": ahead(0, NY - dy, NZ - Z_STEPS[at])},
         )
     landing = returned.at[pl.ds(1, NY * NZ - 1)]
     with jax.named_scope("wait_hits"):
@@ -320,7 +380,7 @@
 
 
 UNROLL = 4
-ABSORB_UNROLL = 2
+ABSORB_UNROLL = 4
 
 
 def place_outputs(result_ref, hits_ref, totals_ref):
@@ -364,14 +424,18 @@
                 pltpu.VMEM((total, width), jnp.bfloat16),
                 pltpu.VMEM((total, LANES), jnp.float32),
                 pltpu.VMEM((3, total, LANES), jnp.float32),
+                pltpu.VMEM((total, LANES), jnp.int32),
+                pltpu.VMEM((NY * NZ, total), jnp.bfloat16),
                 pltpu.VMEM((NY * NZ, 1, LANES), jnp.float32),
                 pltpu.VMEM((NY * NZ, 1, LANES), jnp.float32),
                 pltpu.VMEM((1, LANES), jnp.float32),
                 pltpu.VMEM((pb * NX - 1, 1, LANES), jnp.float32),
                 dma((5,)),
                 dma,
+                dma((NZ,)),
                 dma((PLANE,)),
-                dma((NY,)),
+                dma((2,)),
+                dma((2,)),
                 dma,
                 dma,
                 dma,

time: 35 us -> 32.1 us (0.917)
  Pallas kernels: 34.3 us -> 31.4 us
    pallas_call x1, Pallas kernels: 33.6 us -> 30.7 us  [per_device(): pl.pallas_call(lambda *refs: kernel_body(sizes, *refs), out_shape=pltpu.V...]
where the time goes in v4:
time: 32.1 us; the launch traced here: 32 us
  Pallas kernels  31.4 us (98%)
  between operations  0.64 us (2%)
    pallas_call x1, Pallas kernels, per_device(): pl.pallas_call(lambda *refs: kernel_body(sizes, *refs), out_shape=pltpu.V...  30.7 us
    pallas_call x1, Pallas kernels, per_device(): pl.pallas_call(place_outputs, out_shape=(jax.ShapeDtypeStruct((3, count),...  0.72 us

profile of v4, /device:TPU:1, one launch (start us, length us, event | category | flops | bytes accessed | tf_op | source)
XLA Modules:
  0.0 32.0 jit_solution(9728916197919941390)
XLA Ops:
  0.6 30.7 %recall.1.result_ref = f32[8,128]{1,0:T(8,128)S(1)} custom-call(s32[4]{0:T(128)} %refs_0_.1, bf16[4,1024]{1,0:T(4,128)(2,1)} %refs_1_.1, bf16[1024,1024]{1,0:T(8,128)(2,1)} %refs_2_.1, s32[64,1024]{1,0:T(8,128)} %bitcast.4, f32[64,16,256]{2,1,0:T(8,128)} %bitcast.3), custom_call_target="tpu_custom_call" | custom-call | tf_op jit(solution)/shard_map/recall/pallas_call | solution.py:407
  31.3 0.7 %place.1 = (f32[3,4]{1,0:T(4,128)}, f32[1,3]{1,0:T(1,128)}) custom-call(f32[8,128]{1,0:T(8,128)S(1)} %recall.1.result_ref), custom_call_target="tpu_custom_call" | custom-call | tf_op jit(solution)/shard_map/place/pallas_call | solution.py:449
